TPU v7x, 32 devices: a whole 2x2x4 slice. The times are simulated.
32 devices in a mesh: slab: 8 (over z, y), pencil: 4 (over x, core).
Axes of the slice: x: 2, y: 2, z: 4, core: 2. Of those that a mesh axis runs over, the one named last changes fastest.
Arguments:
- density_history: float32 [7, 64, 320, 320], P(None, 'slab', 'pencil'), may hold values from -6 to 6
- residual_history: float32 [7, 64, 320, 320], P(None, 'slab', 'pencil'), as said below
- occupancy_history: float32 [7, 768, 324], P(None, ('slab', 'pencil')), may hold values from -6 to 6
- occupancy_residual: float32 [7, 768, 324], P(None, ('slab', 'pencil')), may hold values from -6 to 6
- species: int32 [768], P(('slab', 'pencil')), may hold values from 0 to 3
- slot_count: int32 [32], P(('slab', 'pencil')), may hold values from 12 to 24, as said below
Outputs:
- new_density: float32 [64, 320, 320], P('slab', 'pencil')
- new_occupancy: float32 [768, 324], P(('slab', 'pencil'))
Inputs may be any that keep to these rules, and one draw needn't show every extreme that they name: `residual_history`: residual fields of the 7 previous steps. Device d of slab+pencil (slab slowest) holds slots d * 24 to (d + 1) * 24 - 1, of which the first slot_count[d] hold atoms; some device is full in every draw.
All inputs are finite; a program needn't handle non-finite values.
Results may differ from a plain program's by a relative error of at most 0.00017.
Values sent between devices are 32-bit elements; how exact they have to be, the bound alone decides.
A program may use at most 128 MiB of HBM per device.

v0:
```python
import functools
import math

import jax
import jax.numpy as jnp
import numpy as np
from jax import lax
from jax.experimental import pallas as pl
from jax.experimental.pallas import tpu as pltpu
from jax.sharding import PartitionSpec as P

ORBITALS = 18


highest = lax.Precision.HIGHEST
grid_mixing = 0.5
block_mixing = 0.5
kerker_wave = 6.0
species_orbitals = (18, 13, 8, 5)


def block_mask(species, slot_count):
    live = jnp.arange(species.shape[0], dtype=jnp.int32) < slot_count[0]
    orbitals = jnp.zeros_like(species)
    for species_index, orbital_number in enumerate(species_orbitals):
        orbitals = orbitals + orbital_number * (species == species_index).astype(jnp.int32)
    entry = jnp.arange(ORBITALS * ORBITALS, dtype=jnp.int32)
    row_index = entry // ORBITALS
    column_index = entry % ORBITALS
    inside = (
        (row_index[None, :] < orbitals[:, None])
        & (column_index[None, :] < orbitals[:, None])
        & live[:, None]
    )
    return inside.astype(jnp.float32)


def mixing_weights(intersection):
    factor = jnp.linalg.cholesky(intersection)
    column = jnp.ones((intersection.shape[0], 1), intersection.dtype)
    middle = lax.linalg.triangular_solve(factor, column, left_side=True, lower=True)
    solved = lax.linalg.triangular_solve(
        factor, middle, left_side=True, lower=True, transpose_a=True
    )
    return solved[:, 0] / jnp.sum(solved)


def cosine_sine(length, freq_index, space_index):
    product = freq_index * space_index % length
    angle = 2.0 * math.pi / length * product.astype(jnp.float32)
    return (jnp.cos(angle), jnp.sin(angle))


def forward_spectra(fields, pencil_move, slab_move):
    batches, z_local, y_local, x_length = fields.shape
    pencil_count = lax.axis_size("pencil")
    slab_count = lax.axis_size("slab")
    x_columns = x_length // 2
    kx_local = x_columns // pencil_count
    y_length = y_local * pencil_count
    ky_local = y_length // slab_count
    z_length = z_local * slab_count
    freq_index = jnp.arange(x_columns, dtype=jnp.int32).reshape(pencil_count, kx_local, 1)
    space_index = jnp.arange(x_length, dtype=jnp.int32).reshape(1, 1, x_length)
    cosine, sine = cosine_sine(x_length, freq_index, space_index)
    nyquist = cosine_sine(x_length, jnp.full((1, 1, 1), x_length // 2, jnp.int32), space_index)[0]
    sine = jnp.where(freq_index == 0, -nyquist, sine)
    real_part = jnp.einsum("bzyx,pkx->bpkzy", fields, cosine, precision=highest)
    imag_part = -jnp.einsum("bzyx,pkx->bpkzy", fields, sine, precision=highest)
    packed = jnp.stack((real_part, imag_part), axis=1).reshape(batches, 2, pencil_count, -1)
    moved = pencil_move(packed).reshape(batches, 2, pencil_count, kx_local, z_local, y_local)
    freq_index = jnp.arange(y_length, dtype=jnp.int32).reshape(slab_count, ky_local, 1, 1)
    space_index = jnp.arange(y_length, dtype=jnp.int32).reshape(1, 1, pencil_count, y_local)
    cosine, sine = cosine_sine(y_length, freq_index, space_index)
    real_input = moved[:, 0]
    imag_input = moved[:, 1]
    form = "bskzy,glsy->bgklz"
    real_part = jnp.einsum(form, real_input, cosine, precision=highest) + jnp.einsum(
        form, imag_input, sine, precision=highest
    )
    imag_part = jnp.einsum(form, imag_input, cosine, precision=highest) - jnp.einsum(
        form, real_input, sine, precision=highest
    )
    packed = jnp.stack((real_part, imag_part), axis=1).reshape(batches, 2, slab_count, -1)
    moved = slab_move(packed).reshape(batches, 2, slab_count, kx_local, ky_local, z_local)
    freq_index = jnp.arange(z_length, dtype=jnp.int32).reshape(z_length, 1, 1)
    space_index = jnp.arange(z_length, dtype=jnp.int32).reshape(1, slab_count, z_local)
    cosine, sine = cosine_sine(z_length, freq_index, space_index)
    real_input = moved[:, 0]
    imag_input = moved[:, 1]
    form = "bgklz,mgz->bklm"
    real_part = jnp.einsum(form, real_input, cosine, precision=highest) + jnp.einsum(
        form, imag_input, sine, precision=highest
    )
    imag_part = jnp.einsum(form, imag_input, cosine, precision=highest) - jnp.einsum(
        form, real_input, sine, precision=highest
    )
    return jnp.stack((real_part, imag_part), axis=1)


def magnitude(index, length):
    return jnp.minimum(index, length - index).astype(jnp.float32)


def kerker_factor(freq_x, ky_local, x_length, y_length, z_length):
    freq_y = lax.axis_index("slab") * ky_local + jnp.arange(ky_local, dtype=jnp.int32)
    freq_z = jnp.arange(z_length, dtype=jnp.int32)
    square = (
        magnitude(freq_x, x_length)[:, None, None] ** 2
        + magnitude(freq_y, y_length)[None, :, None] ** 2
        + magnitude(freq_z, z_length)[None, None, :] ** 2
    )
    return square / (square + kerker_wave * kerker_wave)


def inverse_field(spectrum, z_local, y_local, x_length):
    pencil_count = lax.axis_size("pencil")
    slab_count = lax.axis_size("slab")
    x_columns = x_length // 2
    kx_local = x_columns // pencil_count
    slots = spectrum.shape[1]
    y_length = y_local * pencil_count
    ky_local = y_length // slab_count
    z_length = z_local * slab_count
    freq_index = jnp.arange(z_length, dtype=jnp.int32).reshape(z_length, 1, 1)
    space_index = jnp.arange(z_length, dtype=jnp.int32).reshape(1, slab_count, z_local)
    cosine, sine = cosine_sine(z_length, freq_index, space_index)
    real_input = spectrum[0]
    imag_input = spectrum[1]
    form = "klm,mdz->dklz"
    real_part = jnp.einsum(form, real_input, cosine, precision=highest) - jnp.einsum(
        form, imag_input, sine, precision=highest
    )
    imag_part = jnp.einsum(form, real_input, sine, precision=highest) + jnp.einsum(
        form, imag_input, cosine, precision=highest
    )
    packed = jnp.stack((real_part, imag_part), axis=0).reshape(2, slab_count, -1)
    moved = lax.all_to_all(packed, "slab", split_axis=1, concat_axis=1, tiled=True).reshape(
        2, slab_count, slots, ky_local, z_local
    )
    freq_index = jnp.arange(y_length, dtype=jnp.int32).reshape(slab_count, ky_local, 1, 1)
    space_index = jnp.arange(y_length, dtype=jnp.int32).reshape(1, 1, pencil_count, y_local)
    cosine, sine = cosine_sine(y_length, freq_index, space_index)
    real_input = moved[0]
    imag_input = moved[1]
    form = "gklz,glqy->qkzy"
    real_part = jnp.einsum(form, real_input, cosine, precision=highest) - jnp.einsum(
        form, imag_input, sine, precision=highest
    )
    imag_part = jnp.einsum(form, real_input, sine, precision=highest) + jnp.einsum(
        form, imag_input, cosine, precision=highest
    )
    packed = jnp.stack((real_part, imag_part), axis=0).reshape(2, pencil_count, -1)
    moved = lax.all_to_all(packed, "pencil", split_axis=1, concat_axis=1, tiled=True).reshape(
        2, pencil_count, slots, z_local, y_local
    )
    pencil_index = jnp.arange(pencil_count, dtype=jnp.int32).reshape(pencil_count, 1, 1)
    slot_index = jnp.arange(slots, dtype=jnp.int32).reshape(1, slots, 1)
    space_index = jnp.arange(x_length, dtype=jnp.int32).reshape(1, 1, x_length)
    freq_index = pencil_index * kx_local + slot_index
    cosine, sine = cosine_sine(x_length, freq_index, space_index)
    nyquist = cosine_sine(x_length, jnp.full((1, 1, 1), x_length // 2, jnp.int32), space_index)[0]
    ordinary = slot_index < kx_local
    doubling = jnp.where(freq_index == 0, 1.0, 2.0)
    real_table = jnp.where(ordinary, doubling * cosine, 0.0)
    imag_table = jnp.where(ordinary, -doubling * sine, jnp.where(pencil_index == 0, nyquist, 0.0))
    form = "pkzy,pkx->zyx"
    field = jnp.einsum(form, moved[0], real_table, precision=highest) + jnp.einsum(
        form, moved[1], imag_table, precision=highest
    )
    return field / (x_length * y_length * z_length)


def body(
    density_history, residual_history, occupancy_history, occupancy_residual, species, slot_count
):
    histories, z_local, y_local, x_length = residual_history.shape
    slab_count = lax.axis_size("slab")
    pencil_count = lax.axis_size("pencil")
    cell_total = z_local * slab_count * y_local * pencil_count * x_length
    slot_total = species.shape[0] * slab_count * pencil_count
    mask = block_mask(species, slot_count)
    flat = residual_history.reshape(histories, -1)
    grid_local = jnp.dot(flat, flat.T, precision=highest) / cell_total
    blocks = (occupancy_residual * mask[None]).reshape(histories, -1)
    block_local = jnp.dot(blocks, blocks.T, precision=highest) / (100.0 * slot_total)
    grid_intersection, block_intersection = lax.psum((grid_local, block_local), ("slab", "pencil"))
    weights = mixing_weights(grid_intersection + block_intersection)
    mixed = jnp.tensordot(weights, residual_history, axes=1, precision=highest)
    spectrum = forward_spectra(
        mixed[None],
        lambda packed: lax.all_to_all(packed, "pencil", split_axis=2, concat_axis=2, tiled=True),
        lambda packed: lax.all_to_all(packed, "slab", split_axis=2, concat_axis=2, tiled=True),
    )[0]
    x_columns = x_length // 2
    kx_local = x_columns // pencil_count
    y_length = y_local * pencil_count
    z_length = z_local * slab_count
    ky_local = y_length // slab_count
    freq_x = lax.axis_index("pencil") * kx_local + jnp.arange(kx_local, dtype=jnp.int32)
    factor = kerker_factor(freq_x, ky_local, x_length, y_length, z_length)
    filtered_spectrum = spectrum * factor[None]
    nyquist_x = jnp.full((1,), x_length // 2, jnp.int32)
    nyquist_factor = kerker_factor(nyquist_x, ky_local, x_length, y_length, z_length)
    owner = (lax.axis_index("pencil") == 0).astype(jnp.float32)
    extra = spectrum[:, 0:1] * nyquist_factor[None] * owner
    filtered_spectrum = jnp.concatenate((filtered_spectrum, extra), axis=1)
    filtered = inverse_field(filtered_spectrum, z_local, y_local, x_length)
    new_density = (
        jnp.tensordot(weights, density_history, axes=1, precision=highest) + grid_mixing * filtered
    )
    mixed_blocks = jnp.tensordot(
        weights, occupancy_history + block_mixing * occupancy_residual, axes=1, precision=highest
    )
    return (new_density, mask * mixed_blocks)


MESH = pl.DeviceIdType.MESH


def split(value):
    high = value.astype(jnp.bfloat16)
    low = (value - high.astype(jnp.float32)).astype(jnp.bfloat16)
    return high, low


def three(left, right, dims):
    numbers = (dims, ((), ()))
    dot = functools.partial(
        lax.dot_general, dimension_numbers=numbers, preferred_element_type=jnp.float32
    )
    return dot(left[1], right[0]) + dot(left[0], right[1]) + dot(left[0], right[0])


def halves(table):
    table = np.asarray(table, np.float32)
    high = table.astype(jnp.bfloat16)
    low = (table - high.astype(np.float32)).astype(jnp.bfloat16)
    return np.stack((high, low))


def waves(rows, columns, length):
    angle = 2.0 * np.pi / length * (np.outer(rows, columns) % length)
    return np.cos(angle), np.sin(angle)


def tables(x_length, y_length, z_length, pencil_count, slab_count, lanes):
    columns = x_length // 2
    cosine, sine = waves(np.arange(columns), np.arange(x_length), x_length)
    nyquist = np.where(np.arange(x_length) % 2 == 0, 1.0, -1.0)
    imag = -sine
    imag[0] = nyquist
    x_forward = np.stack((cosine, imag), axis=1).reshape(x_length, x_length)
    doubling = np.where(np.arange(columns) == 0, 1.0, 2.0)[:, None]
    back = np.stack((doubling * cosine, doubling * imag), axis=1).reshape(x_length, x_length)
    x_back = back * (grid_mixing / (x_length * y_length * z_length))
    cosine, sine = waves(np.arange(y_length), np.arange(y_length), y_length)
    y_local = y_length // pencil_count
    y_forward = np.stack((cosine, sine)).reshape(2, pencil_count, y_local, y_length)
    y_back = np.zeros((2, y_length, pencil_count, lanes))
    y_back[:, :, :, :y_local] = np.stack((cosine, sine)).reshape(2, y_length, pencil_count, y_local)
    y_back = y_back.reshape(2, y_length, pencil_count * lanes)
    cosine, sine = waves(np.arange(z_length), np.arange(z_length), z_length)
    order = np.arange(z_length).reshape(slab_count, -1).T.reshape(-1)
    cosine, sine = cosine[:, order], sine[:, order]
    z_forward = np.block([[cosine, sine], [-sine, cosine]])
    z_back = np.block([[cosine.T, -sine.T], [sine.T, cosine.T]])
    return [halves(t) for t in (x_forward, x_back, y_forward, y_back, z_forward, z_back)]


def pairs_of(count):
    return [(i, j) for i in range(count) for j in range(i + 1)]


def solve_weights(entry, count):
    lower, pivot = {}, []
    for j in range(count):
        scaled = [lower[j, k] * pivot[k] for k in range(j)]
        value = entry[j, j]
        for k in range(j):
            value = value - lower[j, k] * scaled[k]
        pivot.append(value)
        for i in range(j + 1, count):
            value = entry[i, j]
            for k in range(j):
                value = value - lower[i, k] * scaled[k]
            lower[i, j] = value / pivot[j]
    middle = []
    for i in range(count):
        value = jnp.ones_like(pivot[0])
        for k in range(i):
            value = value - lower[i, k] * middle[k]
        middle.append(value)
    solved = [None] * count
    for i in reversed(range(count)):
        value = middle[i] / pivot[i]
        for k in range(i + 1, count):
            value = value - lower[k, i] * solved[k]
        solved[i] = value
    total = solved[0]
    for value in solved[1:]:
        total = total + value
    return [value / total for value in solved]


def mix_kernel(
    slabs, pencils, cells, slots,
    res_hbm, dens_hbm, occ_ref, occ_res_ref, species_ref, live_ref, corner_ref,
    xf_hbm, yf_hbm, yb_hbm, zf_hbm, zb_hbm,
    out_ref, occ_out_ref, field,
    res, dens, sums, send_box, land_box, planes, spectrum, back_box,
    xf_ref, yf_ref, yb_ref, zf_ref, zb_ref,
    load_sem, table_sem, sum_send, sum_recv, go_send, go_recv, back_send, back_recv,
):
    devices = slabs * pencils
    count, z_local, y_local, x_length = res.shape
    slots_k = x_length // 2 // devices
    freqs = 2 * slots_k
    z_length = z_local * slabs
    y_length = y_local * pencils
    lanes = planes.shape[-1]
    tiles_out = send_box.shape[0]
    slab = lax.axis_index("slab")
    pencil = lax.axis_index("pencil")
    me = slab * pencils + pencil
    pairs = pairs_of(count)

    def place(index):
        return (lax.div(index, pencils), lax.rem(index, pencils))

    def other(step):
        return lax.rem(me + step, devices)

    barrier = pltpu.get_barrier_semaphore()

    def greet(step, _):
        pl.semaphore_signal(
            barrier, inc=1, device_id=place(other(step)), device_id_type=MESH
        )
        return 0

    lax.fori_loop(1, devices, greet, 0)

    def load(source, target, which, z):
        return pltpu.make_async_copy(source.at[:, z], target.at[:, z], load_sem.at[which, z])

    for z in range(z_local):
        load(res_hbm, res, 0, z).start()
    from_tables = (xf_hbm, yf_hbm, zf_hbm, zb_hbm, yb_hbm)
    to_tables = (xf_ref, yf_ref, zf_ref, zb_ref, yb_ref)
    loads = [
        pltpu.make_async_copy(a, b, table_sem.at[at])
        for at, (a, b) in enumerate(zip(from_tables, to_tables))
    ]
    for copy in loads:
        copy.start()
    for z in range(z_local):
        load(dens_hbm, dens, 1, z).start()

    limit_shape = (occ_ref.shape[1], 1)
    slot_index = lax.broadcasted_iota(jnp.int32, limit_shape, 0)
    limit = jnp.zeros(limit_shape, jnp.int32)
    for slot in range(occ_ref.shape[1]):
        orbitals = jnp.int32(0)
        for species_index, orbital_number in enumerate(species_orbitals):
            orbitals = jnp.where(species_ref[slot] == species_index, orbital_number, orbitals)
        orbitals = jnp.where(slot < live_ref[0], orbitals, 0)
        limit = jnp.where(slot_index == slot, orbitals, limit)
    mask = (corner_ref[...] < limit).astype(jnp.float32)
    blocks = [occ_res_ref[i] * mask for i in range(count)]
    totals = [
        jnp.sum(blocks[i] * blocks[j], keepdims=True) / (100.0 * slots) for i, j in pairs
    ]
    whole = x_length // 128
    rest = x_length - whole * 128
    for first, width, tiles in ((0, 128, whole), (whole * 128, rest, 1 if rest else 0)):
        if tiles == 0:
            continue
        acc = [jnp.zeros((8, width), jnp.float32) for _ in pairs]
        for z in range(z_local):
            if first == 0:
                load(res_hbm, res, 0, z).wait()

            def rows(step, acc):
                acc = list(acc)
                row = pl.multiple_of(step * 8, 8)
                for t in range(tiles):
                    lane = first + 128 * t
                    part = [res[i, z, pl.ds(row, 8), lane:lane + width] for i in range(count)]
                    for at, (i, j) in enumerate(pairs):
                        acc[at] = acc[at] + part[i] * part[j]
                return tuple(acc)

            acc = lax.fori_loop(0, y_local // 8, rows, tuple(acc))
        totals = [t + jnp.sum(a, keepdims=True) / cells for t, a in zip(totals, acc)]
    lane_index = lax.broadcasted_iota(jnp.int32, (1, 128), 1)
    packed = jnp.zeros((1, 128), jnp.float32)
    for at, value in enumerate(totals):
        packed = jnp.where(lane_index == at, value, packed)
    sums[me] = packed

    pl.semaphore_wait(barrier, devices - 1)

    def sum_copy(step, source):
        return pltpu.make_async_remote_copy(
            src_ref=sums.at[source], dst_ref=sums.at[source],
            send_sem=sum_send.at[step], recv_sem=sum_recv.at[source],
            device_id=place(other(step)), device_id_type=MESH,
        )

    def start_sum(step, _):
        sum_copy(step, me).start()
        return 0

    def wait_sum(step, _):
        sum_copy(step, other(step)).wait_recv()
        return 0

    def drain_sum(step, _):
        sum_copy(step, me).wait_send()
        return 0

    lax.fori_loop(1, devices, start_sum, 0)
    lax.fori_loop(1, devices, wait_sum, 0)
    gathered = sums[0]
    for d in range(1, devices):
        gathered = gathered + sums[d]
    entry = {
        pair: jnp.sum(jnp.where(lane_index == at, gathered, 0.0), axis=1, keepdims=True)
        for at, pair in enumerate(pairs)
    }
    weights = solve_weights(entry, count)

    loads[0].wait()
    x_forward = (xf_ref[0], xf_ref[1])
    rows_out = z_local * y_local
    mixture = []
    for z in range(z_local):
        total = weights[0] * res[0, z]
        for i in range(1, count):
            total = total + weights[i] * res[i, z]
        mixture.append(total)
    turned = three(x_forward, split(jnp.concatenate(mixture, axis=0)), ((1,), (1,)))
    for t in range(tiles_out):
        send_box[t] = turned[:, t * 128:(t + 1) * 128]

    def share(index):
        return pl.ds(index * freqs, freqs)

    def go_copy(step, source, target):
        return pltpu.make_async_remote_copy(
            src_ref=send_box.at[:, share(target), :],
            dst_ref=land_box.at[:, share(source), :],
            send_sem=go_send.at[step], recv_sem=go_recv.at[source],
            device_id=place(target), device_id_type=MESH,
        )

    def start_go(step, _):
        go_copy(step, me, other(step)).start()
        return 0

    def wait_go(step, _):
        go_copy(step, other(step), other(step)).wait_recv()
        return 0

    def drain_go(step, _):
        go_copy(step, me, other(step)).wait_send()
        return 0

    lax.fori_loop(1, devices, start_go, 0)
    land_box[:, share(me), :] = send_box[:, share(me), :]

    for z in range(z_local):
        load(dens_hbm, dens, 1, z).wait()
        total = weights[0] * dens[0, z]
        for i in range(1, count):
            total = total + weights[i] * dens[i, z]
        out_ref[z * y_local:(z + 1) * y_local, :] = total
    total = weights[0] * (occ_ref[0] + block_mixing * occ_res_ref[0])
    for i in range(1, count):
        total = total + weights[i] * (occ_ref[i] + block_mixing * occ_res_ref[i])
    occ_out_ref[...] = mask * total
    lax.fori_loop(1, devices, drain_sum, 0)

    lax.fori_loop(1, devices, wait_go, 0)

    for copy in loads[1:]:
        copy.wait()
    for p in range(pencils):
        for f in range(freqs):
            parts = [
                land_box[t, pl.ds(p * freqs + f, slabs, stride=pencils * freqs), :]
                for t in range(tiles_out)
            ]
            joined = jnp.concatenate(parts, axis=1)
            for z in range(z_local):
                planes[p, f, z * slabs:(z + 1) * slabs, :y_local] = joined[
                    :, z * y_local:(z + 1) * y_local
                ]

    along_cosine, along_sine = None, None
    for p in range(pencils):
        block = split(planes[p].reshape(freqs * z_length, lanes)[:, :y_local])
        cosine = three(block, (yf_ref[0, 0, p], yf_ref[1, 0, p]), ((1,), (0,)))
        sine = three(block, (yf_ref[0, 1, p], yf_ref[1, 1, p]), ((1,), (0,)))
        along_cosine = cosine if p == 0 else along_cosine + cosine
        along_sine = sine if p == 0 else along_sine + sine
    z_forward = (zf_ref[0], zf_ref[1])
    z_back = (zb_ref[0], zb_ref[1])
    shape = (2 * z_length, y_length)
    z_index = lax.rem(lax.broadcasted_iota(jnp.int32, shape, 0), z_length)
    y_index = lax.broadcasted_iota(jnp.int32, shape, 1)
    z_size = jnp.minimum(z_index, z_length - z_index).astype(jnp.float32)
    y_size = jnp.minimum(y_index, y_length - y_index).astype(jnp.float32)
    flat = z_size * z_size + y_size * y_size

    def filtered(wave, freq_x):
        size = freq_x.astype(jnp.float32)
        square = flat + size * size
        return split(wave * (square / (square + kerker_wave * kerker_wave)))

    for k in range(slots_k):
        top, low = 2 * k * z_length, (2 * k + 1) * z_length
        end = low + z_length
        real = along_cosine[top:low] + along_sine[low:end]
        imag = along_cosine[low:end] - along_sine[top:low]
        wave = three(z_forward, split(jnp.concatenate((real, imag), axis=0)), ((1,), (0,)))
        freq_x = me * slots_k + k
        spectrum[k] = three(z_back, filtered(wave, freq_x), ((1,), (0,)))
        if k == 0:
            freq_x = jnp.where(me == 0, x_length // 2, freq_x)
            spectrum[slots_k] = three(z_back, filtered(wave, freq_x), ((1,), (0,)))
    block = split(spectrum[...].reshape((slots_k + 1) * 2 * z_length, y_length))
    along_cosine = three(block, (yb_ref[0, 0], yb_ref[1, 0]), ((1,), (0,)))
    along_sine = three(block, (yb_ref[0, 1], yb_ref[1, 1]), ((1,), (0,)))
    for k in range(slots_k):
        top, low = 2 * k * z_length, (2 * k + 1) * z_length
        end = low + z_length
        real = along_cosine[top:low] - along_sine[low:end]
        if k == 0:
            top, low = 2 * slots_k * z_length, (2 * slots_k + 1) * z_length
            end = low + z_length
        imag = along_cosine[low:end] + along_sine[top:low]
        for c, part in enumerate((real, imag)):
            for p in range(pencils):
                joined = jnp.concatenate(
                    [
                        part[z * slabs:(z + 1) * slabs, p * lanes:p * lanes + y_local]
                        for z in range(z_local)
                    ],
                    axis=1,
                )
                start = p * freqs + 2 * k + c
                for t in range(tiles_out):
                    back_box[t, pl.ds(start, slabs, stride=pencils * freqs), :] = joined[
                        :, t * 128:(t + 1) * 128
                    ]

    def back_copy(step, source, target):
        return pltpu.make_async_remote_copy(
            src_ref=back_box.at[:, share(target), :],
            dst_ref=field.at[:, share(source), :],
            send_sem=back_send.at[step], recv_sem=back_recv.at[source],
            device_id=place(target), device_id_type=MESH,
        )

    def start_back(step, _):
        back_copy(step, me, other(step)).start()
        return 0

    def wait_back(step, _):
        back_copy(step, other(step), other(step)).wait_recv()
        return 0

    def drain_back(step, _):
        back_copy(step, me, other(step)).wait_send()
        return 0

    lax.fori_loop(1, devices, start_back, 0)
    field[:, share(me), :] = back_box[:, share(me), :]
    lax.fori_loop(1, devices, drain_go, 0)
    lax.fori_loop(1, devices, wait_back, 0)
    lax.fori_loop(1, devices, drain_back, 0)


def finish_kernel(field_ref, dens_ref, occ_ref, xb_ref, out_ref, occ_out_ref):
    x_back = (xb_ref[0], xb_ref[1])
    occ_out_ref[...] = occ_ref[...]
    for t in range(field_ref.shape[0]):
        rows = slice(t * 128, (t + 1) * 128)
        out_ref[rows, :] = dens_ref[rows, :] + three(split(field_ref[t]), x_back, ((0,), (0,)))


def fused_body(
    density_history, residual_history, occupancy_history, occupancy_residual, species, slot_count
):
    count, z_local, y_local, x_length = residual_history.shape
    slabs = lax.axis_size("slab")
    pencils = lax.axis_size("pencil")
    devices = slabs * pencils
    z_length, y_length = z_local * slabs, y_local * pencils
    lanes = -(-y_local // 128) * 128
    freqs = x_length // devices
    entry = np.arange(ORBITALS * ORBITALS)
    corner = np.maximum(entry // ORBITALS, entry % ORBITALS)[None].astype(np.int32)
    x_forward, x_back, *others = [
        jnp.asarray(t) for t in tables(x_length, y_length, z_length, pencils, slabs, lanes)
    ]
    constants = [x_forward, *others]
    vmem = pl.BlockSpec(memory_space=pltpu.VMEM)
    smem = pl.BlockSpec(memory_space=pltpu.SMEM)
    hbm = pl.BlockSpec(memory_space=pltpu.HBM)
    box = (z_local * y_local // 128, devices * freqs, 128)
    sems = pltpu.SemaphoreType.DMA
    flat = jax.ShapeDtypeStruct((z_local * y_local, x_length), jnp.float32)
    blocks = jax.ShapeDtypeStruct(occupancy_history.shape[1:], jnp.float32)
    mixed, mixed_blocks, field = pl.pallas_call(
        functools.partial(
            mix_kernel, slabs, pencils,
            z_length * y_length * x_length, species.shape[0] * devices,
        ),
        out_shape=(flat, blocks, jax.ShapeDtypeStruct(box, jnp.float32)),
        in_specs=[hbm, hbm, vmem, vmem, smem, smem, vmem] + [hbm] * 5,
        out_specs=(vmem, vmem, vmem),
        scratch_shapes=[
            pltpu.VMEM(residual_history.shape, jnp.float32),
            pltpu.VMEM(residual_history.shape, jnp.float32),
            pltpu.VMEM((devices, 1, 128), jnp.float32),
            pltpu.VMEM(box, jnp.float32),
            pltpu.VMEM(box, jnp.float32),
            pltpu.VMEM((pencils, freqs, z_length, lanes), jnp.float32),
            pltpu.VMEM((freqs // 2 + 1, 2 * z_length, y_length), jnp.float32),
            pltpu.VMEM(box, jnp.float32),
            *[pltpu.VMEM(t.shape, t.dtype) for t in constants],
            sems((2, z_local)),
            sems((len(constants),)),
            sems((devices,)), sems((devices,)),
            sems((devices,)), sems((devices,)),
            sems((devices,)), sems((devices,)),
        ],
        compiler_params=pltpu.CompilerParams(
            collective_id=0, has_side_effects=True, vmem_limit_bytes=52000 * 1024
        ),
    )(
        residual_history, density_history, occupancy_history, occupancy_residual,
        species, slot_count, jnp.asarray(corner), *constants,
    )
    new_density, new_blocks = pl.pallas_call(
        finish_kernel,
        out_shape=(flat, blocks),
        in_specs=[vmem] * 4,
        out_specs=(vmem, vmem),
        compiler_params=pltpu.CompilerParams(vmem_limit_bytes=20000 * 1024),
    )(field, mixed, mixed_blocks, x_back)
    return new_density.reshape(z_local, y_local, x_length), new_blocks


def solution(mesh):
    placed = (
        P(None, "slab", "pencil", None),
        P(None, "slab", "pencil", None),
        P(None, ("slab", "pencil"), None),
        P(None, ("slab", "pencil"), None),
        P(("slab", "pencil")),
        P(("slab", "pencil")),
    )
    devices = mesh.shape["slab"] * mesh.shape["pencil"]

    def chosen(*arrays):
        x_length = arrays[0].shape[3]
        _, z_local, y_local, _ = arrays[0].shape
        fits = (
            x_length % (2 * devices) == 0
            and mesh.shape["slab"] % 8 == 0
            and y_local % 16 == 0
            and z_local * y_local % 128 == 0
        )
        return (fused_body if fits else body)(*arrays)

    return jax.shard_map(
        chosen,
        mesh=mesh,
        in_specs=placed,
        out_specs=(P("slab", "pencil", None), P(("slab", "pencil"), None)),
        check_vma=False,
    )
```

profile of v0, /device:TPU:31, one launch (start us, length us, event | category | flops | bytes accessed | tf_op | source)
XLA Modules:
  0.0 72.1 jit_solution(8524814146077503969)
XLA Ops:
  1.3 0.0 copy-start.1
  1.3 1.0 %copy-done.1 = bf16[2,320,320]{2,1,0:T(8,128)(2,1)S(1)} copy-done((bf16[2,320,320]{2,1,0:T(8,128)(2,1)S(1)}, bf16[2,320,320]{2,1,0:T(8,128)(2,1)}, u32[]{:S(2)}) %copy-start.1) | copy-done | bytes 409624
  2.3 0.0 copy-start.2
  2.3 0.9 %copy-done.2 = f32[7,24,324]{2,1,0:T(8,128)S(1)} copy-done((f32[7,24,324]{2,1,0:T(8,128)S(1)}, f32[7,24,324]{2,1,0:T(8,128)}, u32[]{:S(2)}) %copy-start.2) | copy-done | bytes 217752
  3.3 0.0 copy-start.3
  3.3 0.9 %copy-done.3 = f32[7,24,324]{2,1,0:T(8,128)S(1)} copy-done((f32[7,24,324]{2,1,0:T(8,128)S(1)}, f32[7,24,324]{2,1,0:T(8,128)}, u32[]{:S(2)}) %copy-start.3) | copy-done | bytes 217752
  4.2 0.0 copy-start.4
  4.2 0.8 %copy-done.4 = bf16[2,128,128]{2,1,0:T(8,128)(2,1)S(1)} copy-done((bf16[2,128,128]{2,1,0:T(8,128)(2,1)S(1)}, bf16[2,128,128]{2,1,0:T(8,128)(2,1)}, u32[]{:S(2)}) %copy-start.4) | copy-done | bytes 65560
  5.0 0.0 copy-start.5
  5.1 0.8 %copy-done.5 = bf16[2,128,128]{2,1,0:T(8,128)(2,1)S(1)} copy-done((bf16[2,128,128]{2,1,0:T(8,128)(2,1)S(1)}, bf16[2,128,128]{2,1,0:T(8,128)(2,1)}, u32[]{:S(2)}) %copy-start.5) | copy-done | bytes 65560
  5.9 0.0 copy-start.6
  5.9 0.7 copy-done.6
  6.6 0.0 copy-start.7
  6.6 0.7 copy-done.7
  7.2 0.0 copy-start
  7.2 62.7 %shard_map.140 = (f32[640,320]{1,0:T(8,128)S(1)}, f32[24,324]{1,0:T(8,128)S(1)}, f32[5,320,128]{2,1,0:T(8,128)S(1)}) custom-call(f32[7,8,80,320]{3,2,1,0:T(8,128)} %res_hbm.1, f32[7,8,80,320]{3,2,1,0:T(8,128)} %dens_hbm.1, f32[7,24,324]{2,1,0:T(8,128)S(1)} %copy-done.2, f32[7,24,324]{2,1,0:T(8,128)S(1)} %copy-done.3, s32[24]{0:T(128)S(1)} %copy-done.7, ...), custom_call_target="tpu_custom_call" | custom-call | tf_op jit(solution)/shard_map/pallas_call | solution.py:617
  69.9 0.0 copy-done
  69.9 2.2 %shard_map.141 = (f32[640,320]{1,0:T(8,128)}, f32[24,324]{1,0:T(8,128)}) custom-call(f32[5,320,128]{2,1,0:T(8,128)S(1)} %get-tuple-element.7.field_ref, f32[640,320]{1,0:T(8,128)S(1)} %get-tuple-element.8.dens_ref, f32[24,324]{1,0:T(8,128)S(1)} %get-tuple-element.9.occ_ref, bf16[2,320,320]{2,1,0:T(8,128)(2,1)S(1)} %copy-done), custom_call_target="tpu_custom_call" | custom-call | tf_op jit(solution)/shard_map/pallas_call | solution.py:648
Async XLA Ops:
  1.3 1.0 %copy-start.1 = (bf16[2,320,320]{2,1,0:T(8,128)(2,1)S(1)}, bf16[2,320,320]{2,1,0:T(8,128)(2,1)}, u32[]{:S(2)}) copy-start(bf16[2,320,320]{2,1,0:T(8,128)(2,1)} %constant.14.clone.xf_hbm) | copy-start | bytes 1228804
  2.3 0.9 %copy-start.2 = (f32[7,24,324]{2,1,0:T(8,128)S(1)}, f32[7,24,324]{2,1,0:T(8,128)}, u32[]{:S(2)}) copy-start(f32[7,24,324]{2,1,0:T(8,128)} %occ_ref.1) | copy-start | bytes 653188
  3.3 0.9 %copy-start.3 = (f32[7,24,324]{2,1,0:T(8,128)S(1)}, f32[7,24,324]{2,1,0:T(8,128)}, u32[]{:S(2)}) copy-start(f32[7,24,324]{2,1,0:T(8,128)} %occ_res_ref.1) | copy-start | bytes 653188
  4.2 0.8 %copy-start.4 = (bf16[2,128,128]{2,1,0:T(8,128)(2,1)S(1)}, bf16[2,128,128]{2,1,0:T(8,128)(2,1)}, u32[]{:S(2)}) copy-start(bf16[2,128,128]{2,1,0:T(8,128)(2,1)} %constant.19.clone.zb_hbm) | copy-start | bytes 196612
  5.0 0.8 %copy-start.5 = (bf16[2,128,128]{2,1,0:T(8,128)(2,1)S(1)}, bf16[2,128,128]{2,1,0:T(8,128)(2,1)}, u32[]{:S(2)}) copy-start(bf16[2,128,128]{2,1,0:T(8,128)(2,1)} %constant.18.clone.zf_hbm) | copy-start | bytes 196612
  5.9 0.7 copy-start.6
  6.6 0.7 copy-start.7
  7.2 62.7 %copy-start = (bf16[2,320,320]{2,1,0:T(8,128)(2,1)S(1)}, bf16[2,320,320]{2,1,0:T(8,128)(2,1)}, u32[]{:S(2)}) copy-start(bf16[2,320,320]{2,1,0:T(8,128)(2,1)} %constant.15.clone.xb_ref) | copy-start | bytes 1228804
where the time goes:
time: 72.7 us; the launch traced here: 72.1 us
  Pallas kernels  64.9 us (89%)
  local copies, waits for them, and re-layouts  5.94 us (8%)
  between operations  1.31 us (2%)
    pallas_call x1, Pallas kernels, fused_body(): pl.pallas_call(functools.partial(mix_kernel, slabs, pencils, z_length * y...  62.7 us
    unnamed x16, local copies, waits for them, and re-layouts  5.94 us
    pallas_call x1, Pallas kernels, fused_body(): pl.pallas_call(finish_kernel, out_shape=(flat, blocks), in_specs=[vmem] *...  2.19 us

commit v1 on v0

--- a/solution.py
+++ b/solution.py
@@ -244,28 +244,33 @@
     return np.cos(angle), np.sin(angle)
 
 
-def tables(x_length, y_length, z_length, pencil_count, slab_count, lanes):
+def tables(x_length, y_length, z_length, pencil_count, slab_count):
     columns = x_length // 2
     cosine, sine = waves(np.arange(columns), np.arange(x_length), x_length)
     nyquist = np.where(np.arange(x_length) % 2 == 0, 1.0, -1.0)
     imag = -sine
     imag[0] = nyquist
-    x_forward = np.stack((cosine, imag), axis=1).reshape(x_length, x_length)
+    slots_k = columns // (pencil_count * slab_count)
+    owner, slot = np.arange(columns) // slots_k, np.arange(columns) % slots_k
+    chunk = np.searchsorted(cuts_of(slots_k), slot, side="right")
+    order = np.lexsort((slot, owner, chunk))
+    x_forward = np.stack((cosine, imag), axis=1)[order].reshape(x_length, x_length)
     doubling = np.where(np.arange(columns) == 0, 1.0, 2.0)[:, None]
-    back = np.stack((doubling * cosine, doubling * imag), axis=1).reshape(x_length, x_length)
+    back = np.stack((doubling * cosine, doubling * imag), axis=1)[order]
+    back = back.reshape(x_length, x_length)
     x_back = back * (grid_mixing / (x_length * y_length * z_length))
     cosine, sine = waves(np.arange(y_length), np.arange(y_length), y_length)
-    y_local = y_length // pencil_count
-    y_forward = np.stack((cosine, sine)).reshape(2, pencil_count, y_local, y_length)
-    y_back = np.zeros((2, y_length, pencil_count, lanes))
-    y_back[:, :, :, :y_local] = np.stack((cosine, sine)).reshape(2, y_length, pencil_count, y_local)
-    y_back = y_back.reshape(2, y_length, pencil_count * lanes)
+    along_y = np.stack((cosine, sine))
     cosine, sine = waves(np.arange(z_length), np.arange(z_length), z_length)
     order = np.arange(z_length).reshape(slab_count, -1).T.reshape(-1)
     cosine, sine = cosine[:, order], sine[:, order]
     z_forward = np.block([[cosine, sine], [-sine, cosine]])
     z_back = np.block([[cosine.T, -sine.T], [sine.T, cosine.T]])
-    return [halves(t) for t in (x_forward, x_back, y_forward, y_back, z_forward, z_back)]
+    return [halves(t) for t in (x_forward, x_back, along_y, z_forward, z_back)]
+
+
+def cuts_of(slots):
+    return [at for at in range(1, slots, 2)] + [slots]
 
 
 def pairs_of(count):
@@ -306,10 +311,10 @@
 def mix_kernel(
     slabs, pencils, cells, slots,
     res_hbm, dens_hbm, occ_ref, occ_res_ref, species_ref, live_ref, corner_ref,
-    xf_hbm, yf_hbm, yb_hbm, zf_hbm, zb_hbm,
+    xf_hbm, yt_hbm, zf_hbm, zb_hbm,
     out_ref, occ_out_ref, field,
     res, dens, sums, send_box, land_box, planes, spectrum, back_box,
-    xf_ref, yf_ref, yb_ref, zf_ref, zb_ref,
+    xf_ref, yt_ref, zf_ref, zb_ref,
     load_sem, table_sem, sum_send, sum_recv, go_send, go_recv, back_send, back_recv,
 ):
     devices = slabs * pencils
@@ -318,7 +323,6 @@
     freqs = 2 * slots_k
     z_length = z_local * slabs
     y_length = y_local * pencils
-    lanes = planes.shape[-1]
     tiles_out = send_box.shape[0]
     slab = lax.axis_index("slab")
     pencil = lax.axis_index("pencil")
@@ -346,8 +350,8 @@
 
     for z in range(z_local):
         load(res_hbm, res, 0, z).start()
-    from_tables = (xf_hbm, yf_hbm, zf_hbm, zb_hbm, yb_hbm)
-    to_tables = (xf_ref, yf_ref, zf_ref, zb_ref, yb_ref)
+    from_tables = (xf_hbm, yt_hbm, zf_hbm, zb_hbm)
+    to_tables = (xf_ref, yt_ref, zf_ref, zb_ref)
     loads = [
         pltpu.make_async_copy(a, b, table_sem.at[at])
         for at, (a, b) in enumerate(zip(from_tables, to_tables))
@@ -432,43 +436,65 @@
     weights = solve_weights(entry, count)
 
     loads[0].wait()
-    x_forward = (xf_ref[0], xf_ref[1])
-    rows_out = z_local * y_local
     mixture = []
     for z in range(z_local):
         total = weights[0] * res[0, z]
         for i in range(1, count):
             total = total + weights[i] * res[i, z]
         mixture.append(total)
-    turned = three(x_forward, split(jnp.concatenate(mixture, axis=0)), ((1,), (1,)))
-    for t in range(tiles_out):
-        send_box[t] = turned[:, t * 128:(t + 1) * 128]
-
-    def share(index):
-        return pl.ds(index * freqs, freqs)
-
-    def go_copy(step, source, target):
+    mixture = split(jnp.concatenate(mixture, axis=0))
+    ends = cuts_of(slots_k)
+    chunks = list(zip([0] + ends[:-1], ends))
+
+    def share(chunk, index):
+        first, end = chunks[chunk]
+        size = 2 * (end - first)
+        return pl.ds(2 * first * devices + index * size, size)
+
+    def go_copy(chunk, step, source, target):
         return pltpu.make_async_remote_copy(
-            src_ref=send_box.at[:, share(target), :],
-            dst_ref=land_box.at[:, share(source), :],
-            send_sem=go_send.at[step], recv_sem=go_recv.at[source],
+            src_ref=send_box.at[:, share(chunk, target), :],
+            dst_ref=land_box.at[:, share(chunk, source), :],
+            send_sem=go_send.at[chunk, step], recv_sem=go_recv.at[chunk, source],
             device_id=place(target), device_id_type=MESH,
         )
 
-    def start_go(step, _):
-        go_copy(step, me, other(step)).start()
-        return 0
-
-    def wait_go(step, _):
-        go_copy(step, other(step), other(step)).wait_recv()
-        return 0
-
-    def drain_go(step, _):
-        go_copy(step, me, other(step)).wait_send()
-        return 0
-
-    lax.fori_loop(1, devices, start_go, 0)
-    land_box[:, share(me), :] = send_box[:, share(me), :]
+    def back_copy(chunk, step, source, target):
+        return pltpu.make_async_remote_copy(
+            src_ref=back_box.at[:, share(chunk, target), :],
+            dst_ref=field.at[:, share(chunk, source), :],
+            send_sem=back_send.at[chunk, step], recv_sem=back_recv.at[chunk, source],
+            device_id=place(target), device_id_type=MESH,
+        )
+
+    def start_all(copy, chunk):
+        def start(step, _):
+            copy(chunk, step, me, other(step)).start()
+            return 0
+
+        lax.fori_loop(1, devices, start, 0)
+
+    def land_all(copy, chunk):
+        def wait(step, _):
+            copy(chunk, step, other(step), other(step)).wait_recv()
+            return 0
+
+        lax.fori_loop(1, devices, wait, 0)
+
+    def drain_all(copy, chunk):
+        def wait(step, _):
+            copy(chunk, step, me, other(step)).wait_send()
+            return 0
+
+        lax.fori_loop(1, devices, wait, 0)
+
+    for chunk, (first, end) in enumerate(chunks):
+        rows = slice(2 * first * devices, 2 * end * devices)
+        turned = three((xf_ref[0, rows, :], xf_ref[1, rows, :]), mixture, ((1,), (1,)))
+        for t in range(tiles_out):
+            send_box[t, rows, :] = turned[:, t * 128:(t + 1) * 128]
+        start_all(go_copy, chunk)
+        land_box[:, share(chunk, me), :] = send_box[:, share(chunk, me), :]
 
     for z in range(z_local):
         load(dens_hbm, dens, 1, z).wait()
@@ -482,31 +508,12 @@
     occ_out_ref[...] = mask * total
     lax.fori_loop(1, devices, drain_sum, 0)
 
-    lax.fori_loop(1, devices, wait_go, 0)
-
     for copy in loads[1:]:
         copy.wait()
-    for p in range(pencils):
-        for f in range(freqs):
-            parts = [
-                land_box[t, pl.ds(p * freqs + f, slabs, stride=pencils * freqs), :]
-                for t in range(tiles_out)
-            ]
-            joined = jnp.concatenate(parts, axis=1)
-            for z in range(z_local):
-                planes[p, f, z * slabs:(z + 1) * slabs, :y_local] = joined[
-                    :, z * y_local:(z + 1) * y_local
-                ]
-
-    along_cosine, along_sine = None, None
-    for p in range(pencils):
-        block = split(planes[p].reshape(freqs * z_length, lanes)[:, :y_local])
-        cosine = three(block, (yf_ref[0, 0, p], yf_ref[1, 0, p]), ((1,), (0,)))
-        sine = three(block, (yf_ref[0, 1, p], yf_ref[1, 1, p]), ((1,), (0,)))
-        along_cosine = cosine if p == 0 else along_cosine + cosine
-        along_sine = sine if p == 0 else along_sine + sine
     z_forward = (zf_ref[0], zf_ref[1])
     z_back = (zb_ref[0], zb_ref[1])
+    y_cosine = (yt_ref[0, 0], yt_ref[1, 0])
+    y_sine = (yt_ref[0, 1], yt_ref[1, 1])
     shape = (2 * z_length, y_length)
     z_index = lax.rem(lax.broadcasted_iota(jnp.int32, shape, 0), z_length)
     y_index = lax.broadcasted_iota(jnp.int32, shape, 1)
@@ -519,68 +526,73 @@
         square = flat + size * size
         return split(wave * (square / (square + kerker_wave * kerker_wave)))
 
-    for k in range(slots_k):
-        top, low = 2 * k * z_length, (2 * k + 1) * z_length
-        end = low + z_length
-        real = along_cosine[top:low] + along_sine[low:end]
-        imag = along_cosine[low:end] - along_sine[top:low]
-        wave = three(z_forward, split(jnp.concatenate((real, imag), axis=0)), ((1,), (0,)))
-        freq_x = me * slots_k + k
-        spectrum[k] = three(z_back, filtered(wave, freq_x), ((1,), (0,)))
-        if k == 0:
-            freq_x = jnp.where(me == 0, x_length // 2, freq_x)
-            spectrum[slots_k] = three(z_back, filtered(wave, freq_x), ((1,), (0,)))
-    block = split(spectrum[...].reshape((slots_k + 1) * 2 * z_length, y_length))
-    along_cosine = three(block, (yb_ref[0, 0], yb_ref[1, 0]), ((1,), (0,)))
-    along_sine = three(block, (yb_ref[0, 1], yb_ref[1, 1]), ((1,), (0,)))
-    for k in range(slots_k):
-        top, low = 2 * k * z_length, (2 * k + 1) * z_length
-        end = low + z_length
-        real = along_cosine[top:low] - along_sine[low:end]
-        if k == 0:
-            top, low = 2 * slots_k * z_length, (2 * slots_k + 1) * z_length
-            end = low + z_length
-        imag = along_cosine[low:end] + along_sine[top:low]
-        for c, part in enumerate((real, imag)):
-            for p in range(pencils):
+    for chunk, (first, end) in enumerate(chunks):
+        size = 2 * (end - first)
+        base = 2 * first * devices
+        land_all(go_copy, chunk)
+        for p in range(pencils):
+            for f in range(size):
                 joined = jnp.concatenate(
                     [
-                        part[z * slabs:(z + 1) * slabs, p * lanes:p * lanes + y_local]
-                        for z in range(z_local)
+                        land_box[t, pl.ds(base + p * size + f, slabs, stride=pencils * size), :]
+                        for t in range(tiles_out)
                     ],
                     axis=1,
                 )
-                start = p * freqs + 2 * k + c
-                for t in range(tiles_out):
-                    back_box[t, pl.ds(start, slabs, stride=pencils * freqs), :] = joined[
-                        :, t * 128:(t + 1) * 128
-                    ]
-
-    def back_copy(step, source, target):
-        return pltpu.make_async_remote_copy(
-            src_ref=back_box.at[:, share(target), :],
-            dst_ref=field.at[:, share(source), :],
-            send_sem=back_send.at[step], recv_sem=back_recv.at[source],
-            device_id=place(target), device_id_type=MESH,
-        )
-
-    def start_back(step, _):
-        back_copy(step, me, other(step)).start()
-        return 0
-
-    def wait_back(step, _):
-        back_copy(step, other(step), other(step)).wait_recv()
-        return 0
-
-    def drain_back(step, _):
-        back_copy(step, me, other(step)).wait_send()
-        return 0
-
-    lax.fori_loop(1, devices, start_back, 0)
-    field[:, share(me), :] = back_box[:, share(me), :]
-    lax.fori_loop(1, devices, drain_go, 0)
-    lax.fori_loop(1, devices, wait_back, 0)
-    lax.fori_loop(1, devices, drain_back, 0)
+                for z in range(z_local):
+                    planes[
+                        2 * first + f, z * slabs:(z + 1) * slabs, p * y_local:(p + 1) * y_local
+                    ] = joined[:, z * y_local:(z + 1) * y_local]
+        block = split(planes[2 * first:2 * end].reshape(size * z_length, y_length))
+        along_cosine = three(block, y_cosine, ((1,), (0,)))
+        along_sine = three(block, y_sine, ((1,), (0,)))
+        extra = first == 0
+        for k in range(first, end):
+            top, low = 2 * (k - first) * z_length, (2 * (k - first) + 1) * z_length
+            stop = low + z_length
+            real = along_cosine[top:low] + along_sine[low:stop]
+            imag = along_cosine[low:stop] - along_sine[top:low]
+            wave = three(z_forward, split(jnp.concatenate((real, imag), axis=0)), ((1,), (0,)))
+            freq_x = me * slots_k + k
+            spectrum[k - first] = three(z_back, filtered(wave, freq_x), ((1,), (0,)))
+            if k == 0:
+                freq_x = jnp.where(me == 0, x_length // 2, freq_x)
+                spectrum[end] = three(z_back, filtered(wave, freq_x), ((1,), (0,)))
+        used = end - first + (1 if extra else 0)
+        block = split(spectrum[0:used].reshape(used * 2 * z_length, y_length))
+        along_cosine = three(block, y_cosine, ((1,), (0,)))
+        along_sine = three(block, y_sine, ((1,), (0,)))
+        for k in range(first, end):
+            top, low = 2 * (k - first) * z_length, (2 * (k - first) + 1) * z_length
+            stop = low + z_length
+            real = along_cosine[top:low] - along_sine[low:stop]
+            if k == 0:
+                top, low = 2 * end * z_length, (2 * end + 1) * z_length
+                stop = low + z_length
+            imag = along_cosine[low:stop] + along_sine[top:low]
+            for c, part in enumerate((real, imag)):
+                for p in range(pencils):
+                    joined = jnp.concatenate(
+                        [
+                            part[z * slabs:(z + 1) * slabs, p * y_local:(p + 1) * y_local]
+                            for z in range(z_local)
+                        ],
+                        axis=1,
+                    )
+                    start = base + p * size + 2 * (k - first) + c
+                    for t in range(tiles_out):
+                        back_box[t, pl.ds(start, slabs, stride=pencils * size), :] = joined[
+                            :, t * 128:(t + 1) * 128
+                        ]
+        start_all(back_copy, chunk)
+        field[:, share(chunk, me), :] = back_box[:, share(chunk, me), :]
+
+    for chunk in range(len(chunks)):
+        drain_all(go_copy, chunk)
+    for chunk in range(len(chunks)):
+        land_all(back_copy, chunk)
+    for chunk in range(len(chunks)):
+        drain_all(back_copy, chunk)
 
 
 def finish_kernel(field_ref, dens_ref, occ_ref, xb_ref, out_ref, occ_out_ref):
@@ -599,14 +611,14 @@
     pencils = lax.axis_size("pencil")
     devices = slabs * pencils
     z_length, y_length = z_local * slabs, y_local * pencils
-    lanes = -(-y_local // 128) * 128
     freqs = x_length // devices
     entry = np.arange(ORBITALS * ORBITALS)
     corner = np.maximum(entry // ORBITALS, entry % ORBITALS)[None].astype(np.int32)
     x_forward, x_back, *others = [
-        jnp.asarray(t) for t in tables(x_length, y_length, z_length, pencils, slabs, lanes)
+        jnp.asarray(t) for t in tables(x_length, y_length, z_length, pencils, slabs)
     ]
     constants = [x_forward, *others]
+    chunks = len(cuts_of(freqs // 2))
     vmem = pl.BlockSpec(memory_space=pltpu.VMEM)
     smem = pl.BlockSpec(memory_space=pltpu.SMEM)
     hbm = pl.BlockSpec(memory_space=pltpu.HBM)
@@ -620,7 +632,7 @@
             z_length * y_length * x_length, species.shape[0] * devices,
         ),
         out_shape=(flat, blocks, jax.ShapeDtypeStruct(box, jnp.float32)),
-        in_specs=[hbm, hbm, vmem, vmem, smem, smem, vmem] + [hbm] * 5,
+        in_specs=[hbm, hbm, vmem, vmem, smem, smem, vmem] + [hbm] * 4,
         out_specs=(vmem, vmem, vmem),
         scratch_shapes=[
             pltpu.VMEM(residual_history.shape, jnp.float32),
@@ -628,18 +640,18 @@
             pltpu.VMEM((devices, 1, 128), jnp.float32),
             pltpu.VMEM(box, jnp.float32),
             pltpu.VMEM(box, jnp.float32),
-            pltpu.VMEM((pencils, freqs, z_length, lanes), jnp.float32),
+            pltpu.VMEM((freqs, z_length, y_length), jnp.float32),
             pltpu.VMEM((freqs // 2 + 1, 2 * z_length, y_length), jnp.float32),
             pltpu.VMEM(box, jnp.float32),
             *[pltpu.VMEM(t.shape, t.dtype) for t in constants],
             sems((2, z_local)),
             sems((len(constants),)),
             sems((devices,)), sems((devices,)),
-            sems((devices,)), sems((devices,)),
-            sems((devices,)), sems((devices,)),
+            sems((chunks, devices)), sems((chunks, devices)),
+            sems((chunks, devices)), sems((chunks, devices)),
         ],
         compiler_params=pltpu.CompilerParams(
-            collective_id=0, has_side_effects=True, vmem_limit_bytes=52000 * 1024
+            collective_id=0, has_side_effects=True, vmem_limit_bytes=56000 * 1024
         ),
     )(
         residual_history, density_history, occupancy_history, occupancy_residual,
@@ -650,7 +662,6 @@
         out_shape=(flat, blocks),
         in_specs=[vmem] * 4,
         out_specs=(vmem, vmem),
-        compiler_params=pltpu.CompilerParams(vmem_limit_bytes=20000 * 1024),
     )(field, mixed, mixed_blocks, x_back)
     return new_density.reshape(z_local, y_local, x_length), new_blocks
 

time: 72.7 us -> 62.3 us (0.86)
  local copies, waits for them, and re-layouts: 5.94 us -> 0 us
  Pallas kernels: 64.9 us -> 60.1 us
    pallas_call x1, Pallas kernels: 62.7 us -> 56.4 us  [fused_body(): pl.pallas_call(functools.partial(mix_kernel, slabs, pencils, z_length * y...]
    unnamed x16 -> x0, local copies, waits for them, and re-layouts: 5.94 us -> none
    pallas_call x1, Pallas kernels: 2.19 us -> 3.73 us  [fused_body(): pl.pallas_call(finish_kernel, out_shape=(flat, blocks), in_specs=[vmem] *...]
where the time goes in v1:
time: 62.3 us; the launch traced here: 61.4 us
  Pallas kernels  60.1 us (96%)
  between operations  1.29 us (2%)
    pallas_call x1, Pallas kernels, fused_body(): pl.pallas_call(functools.partial(mix_kernel, slabs, pencils, z_length * y...  56.4 us
    pallas_call x1, Pallas kernels, fused_body(): pl.pallas_call(finish_kernel, out_shape=(flat, blocks), in_specs=[vmem] *...  3.73 us

profile of v1, /device:TPU:31, one launch (start us, length us, event | category | flops | bytes accessed | tf_op | source)
XLA Modules:
  0.0 61.4 jit_solution(9084574078738650459)
XLA Ops:
  1.3 56.4 %shard_map.131 = (f32[640,320]{1,0:T(8,128)}, f32[24,324]{1,0:T(8,128)}, f32[5,320,128]{2,1,0:T(8,128)}) custom-call(f32[7,8,80,320]{3,2,1,0:T(8,128)} %res_hbm.1, f32[7,8,80,320]{3,2,1,0:T(8,128)} %dens_hbm.1, f32[7,24,324]{2,1,0:T(8,128)} %occ_ref.1, f32[7,24,324]{2,1,0:T(8,128)} %occ_res_ref.1, s32[24]{0:T(128)} %species_ref.1, s32[1]{0:T(128)S(6)} %copy.14.live_ref, ...), custom_call_target="tpu_custom_call" | custom-call | tf_op jit(solution)/shard_map/pallas_call | solution.py:629
  57.7 3.7 %shard_map.132 = (f32[640,320]{1,0:T(8,128)}, f32[24,324]{1,0:T(8,128)}) custom-call(f32[5,320,128]{2,1,0:T(8,128)} %get-tuple-element.7.field_ref, f32[640,320]{1,0:T(8,128)} %get-tuple-element.8.dens_ref, f32[24,324]{1,0:T(8,128)} %get-tuple-element.9.occ_ref, bf16[2,320,320]{2,1,0:T(8,128)(2,1)} %constant.13.clone.xb_ref), custom_call_target="tpu_custom_call" | custom-call | tf_op jit(solution)/shard_map/pallas_call | solution.py:660
